TPU v7x, 256 devices: a whole 4x4x8 slice. The times are simulated.
256 devices in a mesh: seq: 64 (over z, y, core), head: 4 (over x).
Axes of the slice: x: 4, y: 4, z: 8, core: 2. Of those that a mesh axis runs over, the one named last changes fastest.
Arguments:
- tokens: bfloat16 [8192, 2048], P('seq'), may hold values from -20 to 20, as said below
- projection: bfloat16 [2048, 3072], P(None, 'head'), may hold values from -0.078125 to 0.078125
- context_cotangent: bfloat16 [8192, 2048], P('seq', 'head'), may hold values from -80 to 80
Outputs:
- perturbed_context: bfloat16 [8192, 2048], P('seq', 'head')
- ascent_direction: float32 [2048, 3072], P('seq', 'head')
Inputs may be any that keep to these rules, and one draw needn't show every extreme that they name: `tokens`: activations of the layer.
All inputs are finite; a program needn't handle non-finite values.
Results may differ from a plain program's by a relative error of at most 0.017.
Values may be sent and summed in bfloat16 or wider, within the bound.
No kernel may reach another device: no remote copies, remote signals or barrier semaphores. Data moves between devices by JAX's collectives and lax.ppermute only.
A program may use at most 64 MiB of HBM per device.

v0:
```python
import math
import jax
import jax.numpy as jnp
from jax import lax
from jax.sharding import Mesh
from jax.sharding import PartitionSpec as P

INPUT_FEATURES = 2048
KEY_VALUE_HEADS = 4
HEAD_DIMENSION = 128
QUERY_PER_GROUP = 4
SEQ = ("seq_0", "seq_1", "seq_2")
masked_score = -1e30
key_block = 512


def scatter_axes(shard, axes, dim):
    for axis in axes:
        shard = lax.psum_scatter(shard, axis, scatter_dimension=dim, tiled=True)
    return shard


def sent_to_all(shard, axis):
    length = lax.axis_size(axis)
    return lax.all_to_all(
        jnp.broadcast_to(shard[None], (length, *shard.shape)), axis, 0, 0, tiled=True
    )


def taken_together(shard, axis):
    everything = sent_to_all(shard, axis)
    return jnp.sum(everything, axis=0)


def joined_along(tiles, dim):
    tiles = jnp.moveaxis(tiles, 0, dim)
    dims = tiles.shape
    return tiles.reshape(*dims[:dim], dims[dim] * dims[dim + 1], *dims[dim + 2 :])


def stacked_from(shard, axes, turns):
    tiles = shard[None]
    for k in turns:
        tiles = lax.all_gather(tiles, axes[k], axis=0, tiled=True)
    carried = [lax.axis_size(axes[k]) for k in reversed(turns)]
    tiles = tiles.reshape(*carried, *shard.shape)
    turned = sorted(range(len(turns)), key=lambda place: turns[len(turns) - 1 - place])
    return tiles.transpose(*turned, *range(len(turns), tiles.ndim)).reshape(-1, *shard.shape)


def gathered_by_axis(shard, axes, turns, dim):
    return joined_along(stacked_from(shard, axes, turns), dim)


def attend_fold(query_rows, query_pos, score_scale):
    head_size = query_rows.shape[1]

    def single_block(carry_state, block_rows, offset):
        running_max, row_total, context_sum = carry_state
        key_rows = block_rows[:, :head_size]
        value_rows = block_rows[:, head_size:].astype(jnp.float32)
        scores = jnp.dot(query_rows, key_rows.T, preferred_element_type=jnp.float32) * score_scale
        key_pos = offset + jnp.arange(block_rows.shape[0], dtype=jnp.int32)
        allowed = key_pos[None, :] <= query_pos[:, None]
        scores = jnp.where(allowed, scores, masked_score)
        new_max = jnp.maximum(running_max, jnp.max(scores, axis=1))
        factor = jnp.exp(running_max - new_max)
        weights = jnp.where(allowed, jnp.exp(scores - new_max[:, None]), 0.0)
        row_total = row_total * factor + jnp.sum(weights, axis=1)
        context_sum = context_sum * factor[:, None] + jnp.dot(
            weights, value_rows, preferred_element_type=jnp.float32
        )
        return (new_max, row_total, context_sum)

    def fold_keys(carry_state, block_rows, offset):
        row_count = block_rows.shape[0]
        if row_count > key_block and row_count % key_block == 0:

            def sub_block(block_index, inner_state):
                part_rows = lax.dynamic_slice_in_dim(
                    block_rows, block_index * key_block, key_block, 0
                )
                return single_block(inner_state, part_rows, block_index * key_block)

            return lax.fori_loop(0, row_count // key_block, sub_block, carry_state)
        return single_block(carry_state, block_rows, offset)

    return fold_keys


def on_device(tokens, projection, context_cotangent):
    score_scale = HEAD_DIMENSION ** (-0.5)
    local_rows = tokens.shape[0]
    rows_all = local_rows * QUERY_PER_GROUP
    first_row = lax.axis_index(SEQ) * local_rows
    query_pos = first_row + jnp.arange(rows_all, dtype=jnp.int32) // QUERY_PER_GROUP

    def split_heads(projected_weight):
        reshaped_grads = projected_weight.reshape(local_rows, QUERY_PER_GROUP + 2, HEAD_DIMENSION)
        query_rows = reshaped_grads[:, :QUERY_PER_GROUP].reshape(rows_all, HEAD_DIMENSION)
        key_value = reshaped_grads[:, QUERY_PER_GROUP:].reshape(local_rows, 2 * HEAD_DIMENSION)
        return (query_rows, key_value)

    def empty_state():
        return (
            jnp.full((rows_all,), masked_score, jnp.float32),
            jnp.zeros((rows_all,), jnp.float32),
            jnp.zeros((rows_all, HEAD_DIMENSION), jnp.float32),
        )

    projected_weight = jnp.dot(tokens, projection, preferred_element_type=jnp.float32).astype(
        jnp.bfloat16
    )
    query_rows, key_value = split_heads(projected_weight)
    gathered = lax.all_gather(key_value, SEQ, axis=0, tiled=True)
    total_rows = gathered.shape[0]
    block_size = min(key_block, total_rows)
    needed = (first_row + local_rows - 1) // block_size + 1
    fold_first = attend_fold(query_rows, query_pos, score_scale)

    def forward_step(block_index, carry_state):
        block_rows = lax.dynamic_slice_in_dim(gathered, block_index * block_size, block_size, 0)
        return fold_first(carry_state, block_rows, block_index * block_size)

    running_max, row_total, context_sum = lax.fori_loop(0, needed, forward_step, empty_state())
    context = (context_sum / row_total[:, None]).astype(jnp.bfloat16)
    log_total = running_max + jnp.log(row_total)
    grad_rows = context_cotangent.reshape(rows_all, HEAD_DIMENSION)
    row_delta = jnp.sum(grad_rows.astype(jnp.float32) * context.astype(jnp.float32), axis=1)
    contract_rows = (((0,), (0,)), ((), ()))

    def backward_step(block_index, carry_state):
        query_grad, key_terms = carry_state
        offset = block_index * block_size
        block_rows = lax.dynamic_slice_in_dim(gathered, offset, block_size, 0)
        key_rows = block_rows[:, :HEAD_DIMENSION]
        value_rows = block_rows[:, HEAD_DIMENSION:]
        scores = jnp.dot(query_rows, key_rows.T, preferred_element_type=jnp.float32) * score_scale
        key_pos = offset + jnp.arange(block_size, dtype=jnp.int32)
        allowed = key_pos[None, :] <= query_pos[:, None]
        probs_full = jnp.where(allowed, jnp.exp(scores - log_total[:, None]), 0.0)
        probs_half = probs_full.astype(jnp.bfloat16)
        prob_grad = jnp.dot(grad_rows, value_rows.T, preferred_element_type=jnp.float32)
        score_grad = (probs_full * (prob_grad - row_delta[:, None]) * score_scale).astype(
            jnp.bfloat16
        )
        query_grad = query_grad + jnp.dot(score_grad, key_rows, preferred_element_type=jnp.float32)
        key_grad = lax.dot_general(
            score_grad, query_rows, contract_rows, preferred_element_type=jnp.float32
        )
        value_grad = lax.dot_general(
            probs_half, grad_rows, contract_rows, preferred_element_type=jnp.float32
        )
        key_terms = lax.dynamic_update_slice_in_dim(
            key_terms, jnp.concatenate([key_grad, value_grad], axis=1), offset, 0
        )
        return (query_grad, key_terms)

    initial = (
        jnp.zeros((rows_all, HEAD_DIMENSION), jnp.float32),
        jnp.zeros((total_rows, 2 * HEAD_DIMENSION), jnp.float32),
    )
    query_grad, key_terms = lax.fori_loop(0, needed, backward_step, initial)
    key_value_grad = scatter_axes(key_terms, SEQ, 0).astype(jnp.bfloat16)
    head_grads = jnp.concatenate(
        [
            query_grad.astype(jnp.bfloat16).reshape(local_rows, QUERY_PER_GROUP * HEAD_DIMENSION),
            key_value_grad,
        ],
        axis=1,
    )
    grad_term = lax.dot_general(
        tokens, head_grads, contract_rows, preferred_element_type=jnp.float32
    )
    normalizing_scale = math.sqrt(
        INPUT_FEATURES * KEY_VALUE_HEADS * (QUERY_PER_GROUP + 2) * HEAD_DIMENSION
    )
    ascent_radius = 0.2 * math.sqrt(KEY_VALUE_HEADS * (QUERY_PER_GROUP + 2) * HEAD_DIMENSION)
    weight_grad = lax.psum(grad_term, SEQ)
    square_sum = taken_together(jnp.sum(weight_grad * weight_grad), "head")
    grad_norm = jnp.sqrt(square_sum)
    share_rows = INPUT_FEATURES // lax.axis_size(SEQ)
    own_grad = lax.dynamic_slice_in_dim(
        weight_grad, lax.axis_index(SEQ) * share_rows, share_rows, 0
    )
    direction = own_grad * (normalizing_scale / grad_norm)
    moved_weights = (
        projection.astype(jnp.float32) + ascent_radius / grad_norm * weight_grad
    ).astype(jnp.bfloat16)
    projected_new = jnp.dot(tokens, moved_weights, preferred_element_type=jnp.float32).astype(
        jnp.bfloat16
    )
    query_new, key_value_new = split_heads(projected_new)
    fold_new = attend_fold(query_new, query_pos, score_scale)
    final_state = fold_new(
        empty_state(), gathered_by_axis(key_value_new, SEQ, (1, 0, 2), 0), jnp.int32(0)
    )
    perturbed = (
        (final_state[2] / final_state[1][:, None])
        .astype(jnp.bfloat16)
        .reshape(local_rows, QUERY_PER_GROUP * HEAD_DIMENSION)
    )
    return (perturbed, direction)


def solution(mesh):
    finer = Mesh(
        mesh.devices.reshape(8, 4, 2, mesh.shape["head"]), ("seq_0", "seq_1", "seq_2", "head")
    )
    placed = (P(SEQ, None), P(None, "head"), P(SEQ, "head"))
    return jax.shard_map(
        on_device,
        mesh=finer,
        in_specs=placed,
        out_specs=(P(SEQ, "head"), P(SEQ, "head")),
        check_vma=False,
    )
```

profile of v0, /device:TPU:1, one launch (start us, length us, event | category | flops | bytes accessed | tf_op | source)
XLA Modules:
  0.0 723.9 jit_solution(13365416468607866390)
XLA Ops:
  8.2 2.5 convolution_convert_fusion
  12.0 83.2 %all-gather.4.cloned.1.call-done = bf16[8192,256]{1,0:T(8,128)(2,1)} async-done(((bf16[128,256]{1,0:T(8,128)(2,1)}), bf16[8192,256]{1,0:T(8,128)(2,1)}) %all-gather.4.cloned.1.call-update) | async-done | bytes 4194320 | tf_op jit(solution)/shard_map/all_gather | solution.py:115
  95.2 3.0 while.46
  96.8 1.4 convolution_add_fusion.6
  98.5 4.2 broadcast_in_dim.56
  102.7 5.3 while.47
  108.1 214.4 %reduce-scatter.4.cloned.1.call-done = f32[1024,256]{0,1:T(8,128)} async-done(((f32[8192,256]{0,1:T(8,128)}), f32[1024,256]{0,1:T(8,128)}) %reduce-scatter.4.cloned.1.call-update) | async-done | bytes 1048592 | tf_op jit(solution)/shard_map/reduce_scatter | solution.py:19
  322.6 26.0 %reduce-scatter.6.cloned.1.call-done = f32[256,256]{0,1:T(8,128)} async-done(((f32[1024,256]{0,1:T(8,128)}), f32[256,256]{0,1:T(8,128)}) %reduce-scatter.6.cloned.1.call-update) | async-done | bytes 262160 | tf_op jit(solution)/shard_map/reduce_scatter | solution.py:19
  348.8 17.3 %reduce-scatter.8.cloned.1.call-done = f32[128,256]{0,1:T(8,128)} async-done(((f32[256,256]{0,1:T(8,128)}), f32[128,256]{0,1:T(8,128)}) %reduce-scatter.8.cloned.1.call-update) | async-done | bytes 131088 | tf_op jit(solution)/shard_map/reduce_scatter | solution.py:19
  367.1 3.7 convolution_bitcast_fusion
  370.8 4.7 copy.49
  375.5 195.1 %all-reduce.2.cloned.1.call-done = f32[2048,768]{0,1:T(8,128)} async-done(((f32[2048,768]{0,1:T(8,128)}), f32[2048,768]{0,1:T(8,128)}) %all-reduce.2.cloned.1.call-update) | async-done | bytes 6291472 | tf_op jit(solution)/shard_map/psum | solution.py:179
  570.6 5.0 multiply_reduce_fusion
  576.3 7.9 %all_to_all.6 = f32[4,1,1]{2,1,0:T(1,128)S(1)} all-to-all(f32[4,1,1]{2,1,0:T(1,128)S(1)} %broadcast_in_dim.57), channel_id=1, replica_groups=mesh['seq_0'=8,'seq_1'=4,'seq_2'=2,'head'=4] {'head'}, dimensions={0} | all-to-all | bytes 32 | tf_op jit(solution)/shard_map/all_to_all | solution.py:25
  585.5 4.7 fusion.58
  590.4 10.1 %all_gather.13 = bf16[4,128,256]{2,1,0:T(8,128)(2,1)} all-gather(bf16[1,128,256]{2,1,0:T(8,128)(2,1)S(1)} %copy.59), channel_id=1, replica_groups=mesh['seq_0'=8,'seq_1'=4,'seq_2'=2,'head'=4] {'seq_1'}, dimensions={0}, use_global_device_ids=true | all-gather | bytes 327680 | tf_op jit(solution)/shard_map/all_gather | solution.py:44
  600.6 39.3 %all-gather.6.cloned.1.call-done = bf16[32,128,256]{2,1,0:T(8,128)(2,1)} async-done(((bf16[4,128,256]{2,1,0:T(8,128)(2,1)}), bf16[32,128,256]{2,1,0:T(8,128)(2,1)}) %all-gather.6.cloned.1.call-update) | async-done | bytes 2097168 | tf_op jit(solution)/shard_map/all_gather | solution.py:44
  642.1 22.1 %all-gather.8.cloned.1.call-done = bf16[64,128,256]{2,1,0:T(8,128)(2,1)} async-done(((bf16[32,128,256]{2,1,0:T(8,128)(2,1)}), bf16[64,128,256]{2,1,0:T(8,128)(2,1)}) %all-gather.8.cloned.1.call-update) | async-done | bytes 4194320 | tf_op jit(solution)/shard_map/all_gather | solution.py:44
  664.2 4.6 copy.56
  668.8 47.4 %while.48 = (s32[]{:T(128)}, f32[512]{0:T(512)S(1)}, f32[512]{0:T(512)S(1)}, f32[512,128]{1,0:T(8,128)S(1)}, bf16[8192,256]{1,0:T(8,128)(2,1)}, /*index=5*/bf16[...) while((s32[]{:T(128)}, f32[512]{0:T(512)S(1)}, ...), condition=%wide.region_16.17_spmd.clone, body=%wide.region_13.16_spmd.clone.sunk | while | flops 137305600 | bytes 4112599 | solution.py:85
  670.3 1.4 convolution_add_fusion.8
  676.2 1.4 convolution_add_fusion.8
  682.2 1.4 convolution_add_fusion.8
  685.1 1.4 convolution_add_fusion.8
  (168 shorter events, 55.9 us)
Async XLA Ops:
  7.2 1.0 copy-start
  7.2 4.7 copy-start.1
  7.2 88.0 %all-gather.4.cloned.1.call-start = ((), (), s32[]{:S(2)}) async-start(), calls=%async_computation.4 | async-start | bytes 4259840 | tf_op jit(solution)/shard_map/all_gather | solution.py:115
  11.6 310.9 %reduce-scatter.4.cloned.1.call-start = ((), (), s32[]{:S(2)}) async-start(), calls=%async_computation.5 | async-start | bytes 9437184 | tf_op jit(solution)/shard_map/reduce_scatter | solution.py:19
  108.0 240.5 %reduce-scatter.6.cloned.1.call-start = ((), (), s32[]{:S(2)}) async-start(), calls=%async_computation.6 | async-start | bytes 1310720 | tf_op jit(solution)/shard_map/reduce_scatter | solution.py:19
  322.5 43.5 %reduce-scatter.8.cloned.1.call-start = ((), (), s32[]{:S(2)}) async-start(), calls=%async_computation.7 | async-start | bytes 393216 | tf_op jit(solution)/shard_map/reduce_scatter | solution.py:19
  348.6 222.0 %all-reduce.2.cloned.1.call-start = ((), (), s32[]{:S(2)}) async-start(), calls=%async_computation.8 | async-start | bytes 12582912 | tf_op jit(solution)/shard_map/psum | solution.py:179
  370.8 269.1 %all-gather.6.cloned.1.call-start = ((), (), s32[]{:S(2)}) async-start(), calls=%async_computation.9 | async-start | bytes 2359296 | tf_op jit(solution)/shard_map/all_gather | solution.py:44
  600.5 63.6 %all-gather.8.cloned.1.call-start = ((), (), s32[]{:S(2)}) async-start(), calls=%async_computation.10 | async-start | bytes 6291456 | tf_op jit(solution)/shard_map/all_gather | solution.py:44
Sparse Core Ops, SparseCore 0:
  11.8 83.3 all-gather.3
  108.2 214.2 reduce-scatter.3
  325.0 23.4 reduce-scatter.5
  350.9 15.0 reduce-scatter.7
  370.9 199.6 all-reduce.1
  600.6 39.1 all-gather.5
  641.7 22.4 all-gather.7
where the time goes:
time: 726 us; the launch traced here: 724 us
  waiting for transfers between devices  598 us (82%)
  matrix products  60.1 us (8%)
  local copies, waits for them, and re-layouts  18.4 us (3%)
  blocking collectives  18 us (2%)
  between operations  15.1 us (2%)
  other arithmetic  13.5 us (2%)
    reduce_scatter x3, waiting for transfers between devices, scatter_axes(): shard = lax.psum_scatter(shard, axis, scatter_dimension=dim, tiled=True)  258 us
    psum x1, waiting for transfers between devices, on_device(): weight_grad = lax.psum(grad_term, SEQ)  195 us
    all_gather x1, waiting for transfers between devices, on_device(): gathered = lax.all_gather(key_value, SEQ, axis=0, tiled=True)  83.2 us
    all_gather x2, waiting for transfers between devices, stacked_from(): tiles = lax.all_gather(tiles, axes[k], axis=0, tiled=True)  61.4 us
    dot_general x17, matrix products, single_block(): jnp.dot(weights, value_rows, preferred_element_type=jnp.float32)  23.9 us
    dot_general x17, matrix products, single_block(): jnp.dot(query_rows, key_rows.T, preferred_element_type=jnp.float32)  20.9 us
  transfers between devices with their start and end apart: 7, of which 7 were waited for; matrix products, arithmetic and copies ran while one was open for 1% of the time, Pallas kernels for 0%

commit v1 on v0

--- a/solution.py
+++ b/solution.py
@@ -4,6 +4,7 @@
 from jax import lax
 from jax.sharding import Mesh
 from jax.sharding import PartitionSpec as P
+from jax.lax import psum
 
 INPUT_FEATURES = 2048
 KEY_VALUE_HEADS = 4
@@ -176,7 +177,9 @@
         INPUT_FEATURES * KEY_VALUE_HEADS * (QUERY_PER_GROUP + 2) * HEAD_DIMENSION
     )
     ascent_radius = 0.2 * math.sqrt(KEY_VALUE_HEADS * (QUERY_PER_GROUP + 2) * HEAD_DIMENSION)
-    weight_grad = lax.psum(grad_term, SEQ)
+    weight_grad = grad_term
+    for q in ("seq_0", ("seq_1", "seq_2")):
+        weight_grad = psum(weight_grad, q)
     square_sum = taken_together(jnp.sum(weight_grad * weight_grad), "head")
     grad_norm = jnp.sqrt(square_sum)
     share_rows = INPUT_FEATURES // lax.axis_size(SEQ)

time: 726 us -> 766 us (1.055)
  waiting for transfers between devices: 598 us -> 636 us
    psum x1 -> x2, waiting for transfers between devices: 195 us -> 234 us  [on_device(): weight_grad = psum(weight_grad, q)]
  transfers between devices with their start and end apart: 7 -> 8, of which waited for: 7 -> 8; matrix products, arithmetic and copies ran while one was open for 1% -> 1% of each run, Pallas kernels for 0% -> 0%
where the time goes in v1:
time: 766 us; the launch traced here: 763 us
  waiting for transfers between devices  636 us (83%)
  matrix products  60 us (8%)
  local copies, waits for them, and re-layouts  18.4 us (2%)
  blocking collectives  18.4 us (2%)
  between operations  15.1 us (2%)
  other arithmetic  13.5 us (2%)
    reduce_scatter x3, waiting for transfers between devices, scatter_axes(): shard = lax.psum_scatter(shard, axis, scatter_dimension=dim, tiled=True)  258 us
    psum x2, waiting for transfers between devices, on_device(): weight_grad = psum(weight_grad, q)  234 us
    all_gather x1, waiting for transfers between devices, on_device(): gathered = lax.all_gather(key_value, SEQ, axis=0, tiled=True)  83.2 us
    all_gather x2, waiting for transfers between devices, stacked_from(): tiles = lax.all_gather(tiles, axes[k], axis=0, tiled=True)  61.1 us
    dot_general x17, matrix products, single_block(): jnp.dot(weights, value_rows, preferred_element_type=jnp.float32)  23.9 us
    dot_general x17, matrix products, single_block(): jnp.dot(query_rows, key_rows.T, preferred_element_type=jnp.float32)  20.9 us
  transfers between devices with their start and end apart: 8, of which 8 were waited for; matrix products, arithmetic and copies ran while one was open for 1% of the time, Pallas kernels for 0%

profile of v1, /device:TPU:1, one launch (start us, length us, event | category | flops | bytes accessed | tf_op | source)
XLA Modules:
  0.0 763.3 jit_solution(11717293769317625916)
XLA Ops:
  8.2 2.5 convolution_convert_fusion
  12.0 83.2 %all-gather.4.cloned.1.call-done = bf16[8192,256]{1,0:T(8,128)(2,1)} async-done(((bf16[128,256]{1,0:T(8,128)(2,1)}), bf16[8192,256]{1,0:T(8,128)(2,1)}) %all-gather.4.cloned.1.call-update) | async-done | bytes 4194320 | tf_op jit(solution)/shard_map/all_gather | solution.py:116
  95.2 3.0 while.46
  96.8 1.4 convolution_add_fusion.6
  98.5 4.2 broadcast_in_dim.56
  102.7 5.3 while.47
  108.1 214.4 %reduce-scatter.4.cloned.1.call-done = f32[1024,256]{0,1:T(8,128)} async-done(((f32[8192,256]{0,1:T(8,128)}), f32[1024,256]{0,1:T(8,128)}) %reduce-scatter.4.cloned.1.call-update) | async-done | bytes 1048592 | tf_op jit(solution)/shard_map/reduce_scatter | solution.py:20
  322.6 26.0 %reduce-scatter.6.cloned.1.call-done = f32[256,256]{0,1:T(8,128)} async-done(((f32[1024,256]{0,1:T(8,128)}), f32[256,256]{0,1:T(8,128)}) %reduce-scatter.6.cloned.1.call-update) | async-done | bytes 262160 | tf_op jit(solution)/shard_map/reduce_scatter | solution.py:20
  348.8 17.3 %reduce-scatter.8.cloned.1.call-done = f32[128,256]{0,1:T(8,128)} async-done(((f32[256,256]{0,1:T(8,128)}), f32[128,256]{0,1:T(8,128)}) %reduce-scatter.8.cloned.1.call-update) | async-done | bytes 131088 | tf_op jit(solution)/shard_map/reduce_scatter | solution.py:20
  367.1 3.7 convolution_bitcast_fusion
  370.8 148.9 %all-reduce.3.cloned.1.call-done = f32[2048,768]{0,1:T(8,128)} async-done(((f32[2048,768]{0,1:T(8,128)}), f32[2048,768]{0,1:T(8,128)}) %all-reduce.3.cloned.1.call-update) | async-done | bytes 6291472 | tf_op jit(solution)/shard_map/psum | solution.py:182
  519.8 4.7 copy.49
  524.5 85.4 %all-reduce.5.cloned.1.call-done = f32[2048,768]{0,1:T(8,128)} async-done(((f32[2048,768]{0,1:T(8,128)}), f32[2048,768]{0,1:T(8,128)}) %all-reduce.5.cloned.1.call-update) | async-done | bytes 6291472 | tf_op jit(solution)/shard_map/psum | solution.py:182
  609.9 5.0 multiply_reduce_fusion
  615.5 7.9 %all_to_all.6 = f32[4,1,1]{2,1,0:T(1,128)S(1)} all-to-all(f32[4,1,1]{2,1,0:T(1,128)S(1)} %broadcast_in_dim.57), channel_id=1, replica_groups=mesh['seq_0'=8,'seq_1'=4,'seq_2'=2,'head'=4] {'head'}, dimensions={0} | all-to-all | bytes 32 | tf_op jit(solution)/shard_map/all_to_all | solution.py:26
  624.8 4.7 fusion.58
  629.6 10.4 %all_gather.13 = bf16[4,128,256]{2,1,0:T(8,128)(2,1)} all-gather(bf16[1,128,256]{2,1,0:T(8,128)(2,1)S(1)} %copy.59), channel_id=1, replica_groups=mesh['seq_0'=8,'seq_1'=4,'seq_2'=2,'head'=4] {'seq_1'}, dimensions={0}, use_global_device_ids=true | all-gather | bytes 327680 | tf_op jit(solution)/shard_map/all_gather | solution.py:45
  640.1 39.1 %all-gather.6.cloned.1.call-done = bf16[32,128,256]{2,1,0:T(8,128)(2,1)} async-done(((bf16[4,128,256]{2,1,0:T(8,128)(2,1)}), bf16[32,128,256]{2,1,0:T(8,128)(2,1)}) %all-gather.6.cloned.1.call-update) | async-done | bytes 2097168 | tf_op jit(solution)/shard_map/all_gather | solution.py:45
  681.4 22.1 %all-gather.8.cloned.1.call-done = bf16[64,128,256]{2,1,0:T(8,128)(2,1)} async-done(((bf16[32,128,256]{2,1,0:T(8,128)(2,1)}), bf16[64,128,256]{2,1,0:T(8,128)(2,1)}) %all-gather.8.cloned.1.call-update) | async-done | bytes 4194320 | tf_op jit(solution)/shard_map/all_gather | solution.py:45
  703.5 4.6 copy.56
  708.1 47.4 %while.48 = (s32[]{:T(128)}, f32[512]{0:T(512)S(1)}, f32[512]{0:T(512)S(1)}, f32[512,128]{1,0:T(8,128)S(1)}, bf16[8192,256]{1,0:T(8,128)(2,1)}, /*index=5*/bf16[...) while((s32[]{:T(128)}, f32[512]{0:T(512)S(1)}, ...), condition=%wide.region_17.18_spmd.clone, body=%wide.region_14.17_spmd.clone.sunk | while | flops 137305600 | bytes 4112599 | solution.py:86
  709.7 1.4 convolution_add_fusion.8
  715.6 1.4 convolution_add_fusion.8
  721.5 1.4 convolution_add_fusion.8
  (171 shorter events, 57.4 us)
Async XLA Ops:
  7.2 1.0 copy-start
  7.2 4.7 copy-start.1
  7.2 88.0 %all-gather.4.cloned.1.call-start = ((), (), s32[]{:S(2)}) async-start(), calls=%async_computation.4 | async-start | bytes 4259840 | tf_op jit(solution)/shard_map/all_gather | solution.py:116
  11.6 310.9 %reduce-scatter.4.cloned.1.call-start = ((), (), s32[]{:S(2)}) async-start(), calls=%async_computation.5 | async-start | bytes 9437184 | tf_op jit(solution)/shard_map/reduce_scatter | solution.py:20
  108.0 240.5 %reduce-scatter.6.cloned.1.call-start = ((), (), s32[]{:S(2)}) async-start(), calls=%async_computation.6 | async-start | bytes 1310720 | tf_op jit(solution)/shard_map/reduce_scatter | solution.py:20
  322.5 43.5 %reduce-scatter.8.cloned.1.call-start = ((), (), s32[]{:S(2)}) async-start(), calls=%async_computation.7 | async-start | bytes 393216 | tf_op jit(solution)/shard_map/reduce_scatter | solution.py:20
  348.6 171.1 %all-reduce.3.cloned.1.call-start = ((), (), s32[]{:S(2)}) async-start(), calls=%async_computation.8 | async-start | bytes 12582912 | tf_op jit(solution)/shard_map/psum | solution.py:182
  370.8 239.1 %all-reduce.5.cloned.1.call-start = ((), (), s32[]{:S(2)}) async-start(), calls=%async_computation.9 | async-start | bytes 12582912 | tf_op jit(solution)/shard_map/psum | solution.py:182
  519.8 159.5 %all-gather.6.cloned.1.call-start = ((), (), s32[]{:S(2)}) async-start(), calls=%async_computation.10 | async-start | bytes 2359296 | tf_op jit(solution)/shard_map/all_gather | solution.py:45
  640.1 63.4 %all-gather.8.cloned.1.call-start = ((), (), s32[]{:S(2)}) async-start(), calls=%async_computation.11 | async-start | bytes 6291456 | tf_op jit(solution)/shard_map/all_gather | solution.py:45
Sparse Core Ops, SparseCore 0:
  11.8 83.3 all-gather.3
  108.2 214.2 reduce-scatter.3
  325.0 23.4 reduce-scatter.5
  350.9 15.0 reduce-scatter.7
  370.9 148.8 all-reduce.2
  522.0 87.8 all-reduce.4
  640.2 38.9 all-gather.5
  681.0 22.4 all-gather.7
